TPU v7x, 256 devices: a 8x8x2 block of a 8x8x16 slice. The times are simulated.
256 devices in a mesh: groups: 2 (over z), blk: 16 (over y, core), col: 8 (over x).
Axes of the slice: x: 8, y: 8, z: 2, core: 2. Of those that a mesh axis runs over, the one named last changes fastest.
The devices are a block of a 8x8x16 slice.
Arguments:
- pair_block: bfloat16 [4096, 16384], P(('groups', 'blk'), 'col'), parts along dimension 0, may hold values from -1.5 to 1.5
- occ_energy: float32 [2], P('groups'), parts along dimension 0, may hold values from -1.5 to -0.3
- virt_energy: float32 [4096], P('groups'), parts along dimension 0, may hold values from 0.2 to 3
- frequency: float32 [2], P('groups'), parts along dimension 0, may hold values from 0.2 to 2
Outputs:
- dielectric: float32 [32768, 16384], P(('groups', 'col'), 'blk'), parts along dimension 0
There are 2 independent parts, one for each index of `groups`. A program takes and returns all parts, laid end to end along the dimension named above; each array names one. Nothing has to cross between parts.
All inputs are finite; a program needn't handle non-finite values.
Results may differ from a plain program's by a relative error of at most 0.0027.
Values may be sent and summed in bfloat16 or wider, within the bound.
A program may use at most 64 MiB of HBM per device.

v0:
```python
import jax
import jax.numpy as jnp
from jax import lax
from jax.sharding import PartitionSpec as P


def spread(value, axis, source):
    kept = jnp.where(lax.axis_index(axis) == source, value, 0).astype(value.dtype)
    return lax.psum(kept, axis)


def pair_weights(occ_energy, virt_energy, frequency):
    gap = (virt_energy[None, :] - occ_energy[:, None]).reshape(-1)
    return 2.0 * gap / (gap * gap + frequency[0] * frequency[0])


def shards(pair_block, occ_energy, virt_energy, frequency):
    rows_dev, cols_dev = pair_block.shape
    blk_count = lax.axis_size("blk")
    naux_total = cols_dev * lax.axis_size("col")
    slab_width = naux_total // blk_count
    blk_index = lax.axis_index("blk")
    weights = pair_weights(occ_energy, virt_energy, frequency)
    gathered = lax.all_gather(pair_block, "blk", axis=0, tiled=True)
    first_col = blk_index * slab_width
    owner_index = first_col // cols_dev
    offset = first_col % cols_dev
    own_slab = lax.dynamic_slice_in_dim(gathered, offset, slab_width, 1)
    column_slab = spread(own_slab, "col", owner_index)
    scaled = (gathered.astype(jnp.float32) * weights[:, None]).astype(jnp.bfloat16)
    result_tile = lax.dot_general(
        scaled, column_slab, (((0,), (0,)), ((), ())), preferred_element_type=jnp.float32
    )
    return result_tile


def solution(mesh):
    return jax.shard_map(
        shards,
        mesh=mesh,
        in_specs=(P(("groups", "blk"), "col"), P("groups"), P("groups"), P("groups")),
        out_specs=P(("groups", "col"), "blk"),
        check_vma=False,
    )
```

profile of v0, /device:TPU:514, one launch (start us, length us, event | category | flops | bytes accessed | tf_op | source)
XLA Modules:
  0.0 220.5 jit_solution(5214615519437316589)
XLA Ops:
  6.5 0.0 copy-start
  6.5 0.0 all-gather.2.cloned.1.call-start
  6.6 0.7 all-gather.2.cloned.1.call-update
  7.3 0.1 all-reduce.2.cloned.1.call-start
  7.4 76.9 %all-gather.2.cloned.1.call-done = bf16[2048,2048]{1,0:T(8,128)(2,1)} async-done(((bf16[128,2048]{1,0:T(8,128)(2,1)}), bf16[2048,2048]{1,0:T(8,128)(2,1)}) %all-gather.2.cloned.1.call-update) | async-done | bytes 8388624 | tf_op jit(solution)/shard_map/all_gather | solution.py:24
  84.3 5.4 %dynamic-slice_select_fusion = bf16[2048,1024]{1,0:T(8,128)(2,1)} fusion(bf16[2048,2048]{1,0:T(8,128)(2,1)} %all-gather.2.cloned.1.call-done, s32[]{:T(128)S(6)} %select_n.25, pred[]{:T(512)S(6)} %eq.5), kind=kLoop, calls=%fused_computation.3 | loop fusion | flops 2097152 | bytes 8388613 | tf_op jit(solution)/shard_map/jit(_where)/select_n | solution.py:8
  89.7 0.1 all-reduce.2.cloned.1.call-update
  91.1 0.0 copy-done
  91.1 107.6 %all-reduce.2.cloned.1.call-done = bf16[2048,1024]{1,0:T(8,128)(2,1)} async-done(((bf16[2048,1024]{1,0:T(8,128)(2,1)}), bf16[2048,1024]{1,0:T(8,128)(2,1)}) %all-reduce.2.cloned.1.call-update) | async-done | bytes 4194320 | tf_op jit(solution)/shard_map/psum | solution.py:9
  198.7 14.9 %fusion = f32[2048,1024]{1,0:T(8,128)} fusion(bf16[2048,1024]{1,0:T(8,128)(2,1)} %all-reduce.2.cloned.1.call-done, bf16[2048,2048]{1,0:T(8,128)(2,1)} %all-gather.2.cloned.1.call-done, f32[2048]{0:T(1024)S(1)} %add_divide_fusion), kind=kOutput, calls=%fused_computation.1 | convolution fusion | flops 8602517504 | bytes 20979712 | tf_op jit(solution)/shard_map/dot_general | solution.py:31
  (1 shorter events, 0.0 us)
Async XLA Ops:
  6.5 84.5 %copy-start = (f32[2048]{0:T(1024)S(1)}, f32[2048]{0:T(1024)}, u32[]{:S(2)}) copy-start(f32[2048]{0:T(1024)} %param.6) | copy-start | bytes 24580
  6.5 77.8 %all-gather.2.cloned.1.call-start = ((), (), s32[]{:S(2)}) async-start(), calls=%async_computation | async-start | bytes 8912896 | tf_op jit(solution)/shard_map/all_gather | solution.py:24
  7.3 191.4 %all-reduce.2.cloned.1.call-start = ((), (), s32[]{:S(2)}) async-start(), calls=%async_computation.1 | async-start | bytes 8388608 | tf_op jit(solution)/shard_map/psum | solution.py:9
Sparse Core Ops, SparseCore 0:
  9.2 75.0 all-gather.1
  89.9 108.7 all-reduce.1
where the time goes:
time: 223 us; the launch traced here: 220 us
  waiting for transfers between devices  185 us (83%)
  matrix products  14.9 us (7%)
  between operations  14.8 us (7%)
  other arithmetic  5.43 us (2%)
    psum x1, waiting for transfers between devices, spread(): return lax.psum(kept, axis)  108 us
    all_gather x1, waiting for transfers between devices, shards(): gathered = lax.all_gather(pair_block, 'blk', axis=0, tiled=True)  76.9 us
    dot_general x1, matrix products, shards(): lax.dot_general(scaled, column_slab, (((0,), (0,)), ((), ())), preferred_...  14.9 us
    select_n x1, other arithmetic, spread(): jnp.where(lax.axis_index(axis) == source, value, 0).astype(value.dtype)  5.42 us
  transfers between devices with their start and end apart: 2, of which 2 were waited for; matrix products, arithmetic and copies ran while one was open for 0% of the time, Pallas kernels for 0%

commit v1 on v0

v1 whole, which is shorter than its diff:
```python
import functools

import jax
import jax.numpy as jnp
from jax import lax
from jax.experimental import pallas as pl
from jax.experimental.pallas import tpu as pltpu
from jax.sharding import PartitionSpec as P

MESH = pl.DeviceIdType.MESH
CORES = 2
SUB = 4
LAG = 4
HOP = 2


def element(e, up, row, n):
    half = SUB
    g = e + half
    dist, within = g // (CORES * SUB), g % (CORES * SUB)
    sub = within // CORES - jnp.where(dist == 0, SUB // 2, 0)
    sub = jnp.where(up, sub, SUB - 1 - sub)
    chip = (row + jnp.where(up, n - dist, dist)) % n
    return chip, sub, within % CORES


def schedule(n):
    total = n * CORES * SUB
    end = total // 2 + n // 2 * HOP
    table = []
    for pos in range(n):
        ready = {}
        for d in range(-(n // 2 - 1), n // 2 + 1):
            if d == 0:
                ready[d] = 1
            elif d == n // 2:
                ready[d] = LAG + 1 + 2 * (SUB * (n // 2 - 1) + SUB // 2 - 1)
            else:
                ready[d] = LAG + 1 + 2 * (SUB * abs(d) - 1)
        if pos:
            for e in range(total // 2):
                g = e + SUB
                dist = g // (CORES * SUB)
                for up in (True, False):
                    first, last = (pos, n - pos) if up else (n - pos, pos)
                    tick = e + first * HOP if e + first * HOP < end else total - 1 - e + last * HOP
                    key = dist if up else -dist
                    if dist == n // 2:
                        key = dist
                    ready[key] = max(ready[key], tick)
        order = sorted(ready, key=lambda d: (ready[d], abs(d), d))
        starts, free = [], 0
        for d in order[:-1]:
            free = max(free, ready[d])
            starts.append(free)
            free += 2
        table.append((order, starts))
    return end, table


def pick(index, values):
    out = jnp.int32(values[0])
    for k in range(1, len(values)):
        out = jnp.where(index == k, jnp.int32(values[k]), out)
    return out


def gather_kernel(n, block_ref, weight_ref, acc, last_lhs, last_rhs, held, load_sem,
                  y_send, y_recv, d_send, d_recv, x_send, x_recv):
    rows, cols = block_ref.shape
    piece = rows // SUB
    slab = cols // CORES
    tile = CORES * rows
    tiles = cols // tile
    b = lax.axis_index("blk")
    x = lax.axis_index("col")
    core, y = b % CORES, b // CORES
    other = 1 - core
    total = n * CORES * SUB
    end, table = schedule(n)
    send_end = end - HOP
    y_count = SUB * (n // 2 - 1) + SUB // 2
    pos = (x - y + n) % n

    peer = {"blk": y * CORES + other}
    chip_y = ({"blk": ((y + 1) % n) * CORES + core}, {"blk": ((y + n - 1) % n) * CORES + core})
    chip_x = ({"col": (x + 1) % n}, {"col": (x + n - 1) % n})

    load = pltpu.make_async_copy(
        block_ref, held.at[y, pl.ds(pl.multiple_of(core * rows, rows), rows), pl.ds(0, cols)], load_sem)
    load.start()
    barrier = pltpu.get_barrier_semaphore()
    for device in (peer,) + chip_y + chip_x:
        pl.semaphore_signal(barrier, inc=1, device_id=device, device_id_type=MESH)
    pl.semaphore_wait(barrier, 5)
    load.wait()

    def rows_of(owner, sub):
        return pl.ds(pl.multiple_of(owner * rows + sub * piece, piece), piece)

    def full(chip, owner, sub):
        return held.at[chip, rows_of(owner, sub), pl.ds(0, cols)]

    def copy(src, dst, send, recv, device):
        return pltpu.make_async_remote_copy(src_ref=src, dst_ref=dst, send_sem=send, recv_sem=recv,
                                            device_id=device, device_id_type=MESH)

    def y_copy(way, j):
        d, k = j // SUB, j % SUB
        chip = (y + (n - d if way == 0 else d)) % n
        ref = full(chip, core, k if way == 0 else SUB - 1 - k)
        return copy(ref, ref, y_send.at[way, j], y_recv.at[way, j], chip_y[way])

    def y_arrival(way, j):
        d, k = j // SUB + 1, j % SUB
        chip = (y + (n - d if way == 0 else d)) % n
        return chip, k if way == 0 else SUB - 1 - k

    def d_copy(way, j, owner):
        chip, sub = y_arrival(way, j)
        ref = full(chip, owner, sub)
        return copy(ref, ref, d_send.at[way, j], d_recv.at[way, j], peer)

    def own_copy(k, owner):
        ref = full(y, owner, k)
        return copy(ref, ref, d_send.at[2, k], d_recv.at[2, k], peer)

    for k in range(SUB):
        for way in (0, 1):
            y_copy(way, k).start()
    for k in range(SUB):
        own_copy(k, core).start()

    zero = jnp.zeros((tile, slab), jnp.float32)

    def clear(m, carry):
        acc[pl.ds(pl.multiple_of(m * tile, tile), tile), :] = zero
        return carry

    lax.fori_loop(0, tiles, clear, 0)

    landing = pl.ds(cols, slab)
    source = pl.ds(pl.multiple_of(jnp.where(pos == 0, core * slab, cols), slab), slab)
    hops = (pos, (n - pos) % n)

    def x_copy(way, i):
        up = (i < total // 2) if way == 0 else (i >= total // 2)
        chip, sub, swap = element(jnp.where(i < total // 2, i, total - 1 - i), up, y, n)
        owner = (core + swap) % CORES
        at = rows_of(owner, sub)
        return copy(held.at[chip, at, source], held.at[chip, at, landing],
                    x_send.at[way, i], x_recv.at[way, i], chip_x[way])

    def x_sends(way, t):
        i = t - hops[way] * HOP
        return (i >= 0) & (t < send_end) & (hops[way] != n - 1), i

    def x_step(t):
        for way in (0, 1):
            i = t - hops[way] * HOP

            @pl.when((i >= 0) & (t < end) & (hops[way] != 0))
            def _():
                x_copy(way, i).wait_recv()

            @pl.when((i >= 0) & (t < send_end) & (hops[way] != n - 1))
            def _():
                x_copy(way, i).start()

    order = [pick(pos, [o[s] for o, _ in table]) for s in range(n)]
    starts = [pick(pos, [s[k] for _, s in table]) for k in range(n - 1)]
    steps = max(s[-1] for _, s in table) + 2
    steps += steps % 2

    def scaled(chip, m):
        part = held[chip, :, pl.ds(pl.multiple_of(m * tile, tile), tile)].T
        return (part.astype(jnp.float32) * weight_ref[pl.ds(chip, 1), :]).astype(jnp.bfloat16)

    def multiply(t):
        work = jnp.int32(-1)
        dist = jnp.int32(0)
        for k in range(n - 1):
            here = (t == starts[k]) | (t == starts[k] + 1)
            work = jnp.where(here, t - starts[k], work)
            dist = jnp.where(here, order[k], dist)

        @pl.when(work >= 0)
        def _():
            chip = (y + n - dist) % n

            def one(m, carry):
                at = pl.ds(pl.multiple_of(m * tile, tile), tile)
                acc[at, :] += jnp.dot(scaled(chip, m), held[chip, :, source], preferred_element_type=jnp.float32)
                return carry

            lax.fori_loop(work * (tiles // 2), (work + 1) * (tiles // 2), one, 0)

    final = (y + n - order[n - 1]) % n

    def pair(h, carry):
        t = 2 * h
        j = h - LAG // 2

        @pl.when((j >= 0) & (j < y_count))
        def _():
            for way in (0, 1):
                y_copy_in = d_copy(way, j, core)
                chip, sub = y_arrival(way, j)
                ref = full(chip, core, sub)
                copy(ref, ref, y_send.at[way, j], y_recv.at[way, j], chip_y[way]).wait_recv()

                @pl.when(j + SUB < y_count)
                def _():
                    y_copy(way, j + SUB).start()

                y_copy_in.start()

        x_step(t)
        multiply(t)

        @pl.when(h == 0)
        def _():
            for k in range(SUB):
                own_copy(k, other).wait_recv()

        @pl.when((j >= 0) & (j < y_count))
        def _():
            for way in (0, 1):
                d_copy(way, j, other).wait_recv()

        x_step(t + 1)
        multiply(t + 1)

        @pl.when(h == (end - 4) // 2)
        def _():
            def one(m, carry):
                last_lhs[pl.ds(pl.multiple_of(m * tile, tile), tile), :] = scaled(final, m)
                return carry

            lax.fori_loop(0, tiles, one, 0)

        return carry

    lax.fori_loop(0, steps // 2, pair, 0)
    last_rhs[...] = held[final, :, source]

    def drain_y(j, carry):
        for way in (0, 1):
            y_copy(way, j).wait_send()
            d_copy(way, j, core).wait_send()
        return carry

    lax.fori_loop(0, y_count, drain_y, 0)
    for k in range(SUB):
        own_copy(k, core).wait_send()

    def drain_x(t, carry):
        for way in (0, 1):
            sent, i = x_sends(way, t)

            @pl.when(sent)
            def _():
                x_copy(way, i).wait_send()
        return carry

    lax.fori_loop(0, send_end, drain_x, 0)


def finish_kernel(acc, lhs, rhs, out_ref, staged, sems):
    tiles = sems.shape[0]
    tile = acc.shape[0] // tiles
    copies = []
    for m in range(tiles):
        at = pl.ds(m * tile, tile)
        staged[at, :] = acc[at, :] + jnp.dot(lhs[at, :], rhs[...], preferred_element_type=jnp.float32)
        out = pltpu.make_async_copy(staged.at[at], out_ref.at[at], sems.at[m])
        out.start()
        copies.append(out)
    for out in copies:
        out.wait()


def shards(pair_block, occ_energy, virt_energy, frequency):
    rows, cols = pair_block.shape
    n = lax.axis_size("col")
    assert lax.axis_size("blk") == CORES * n
    slab = cols // CORES
    tile = CORES * rows
    gap = (virt_energy[None, :] - occ_energy[:, None]).reshape(-1)
    weights = (2.0 * gap / (gap * gap + frequency[0] * frequency[0])).reshape(n, tile)
    end, _ = schedule(n)
    y_count = SUB * (n // 2 - 1) + SUB // 2
    dma = pltpu.SemaphoreType.DMA
    vmem = pl.BlockSpec(memory_space=pltpu.VMEM)
    acc, lhs, rhs = pl.pallas_call(
        functools.partial(gather_kernel, n),
        out_shape=(pltpu.VMEM((cols, slab), jnp.float32), pltpu.VMEM((cols, tile), jnp.bfloat16),
                   pltpu.VMEM((tile, slab), jnp.bfloat16)),
        in_specs=[pl.BlockSpec(memory_space=pl.ANY), vmem],
        out_specs=(vmem, vmem, vmem),
        scratch_shapes=[
            pltpu.VMEM((n, tile, cols + slab), jnp.bfloat16),
            dma,
            dma((2, y_count)), dma((2, y_count)),
            dma((3, y_count)), dma((3, y_count)),
            dma((2, end)), dma((2, end)),
        ],
        compiler_params=pltpu.CompilerParams(collective_id=0, has_side_effects=True, vmem_limit_bytes=20 * 2**20),
    )(pair_block, weights)
    return pl.pallas_call(
        finish_kernel,
        out_shape=jax.ShapeDtypeStruct((cols, slab), jnp.float32),
        in_specs=[vmem, vmem, vmem],
        out_specs=pl.BlockSpec(memory_space=pl.ANY),
        scratch_shapes=[pltpu.VMEM((cols, slab), jnp.float32), dma((n,))],
        compiler_params=pltpu.CompilerParams(vmem_limit_bytes=20 * 2**20),
    )(acc, lhs, rhs)


def solution(mesh):
    return jax.shard_map(
        shards,
        mesh=mesh,
        in_specs=(P(("groups", "blk"), "col"), P("groups"), P("groups"), P("groups")),
        out_specs=P(("groups", "col"), "blk"),
        check_vma=False,
    )
```

time: 223 us -> 105 us (0.47)
  waiting for transfers between devices: 185 us -> 0 us
  Pallas kernels: 0 us -> 100 us
  matrix products: 14.9 us -> 0 us
  between operations: 14.8 us -> 1.31 us
  other arithmetic: 5.43 us -> 0.71 us
    psum x1 -> x0, waiting for transfers between devices: 108 us -> none  [spread(): return lax.psum(kept, axis)]
    pallas_call x0 -> x2, Pallas kernels: none -> 100 us  [the longest x1 96.8 us: shards(): pl.pallas_call(functools.partial(gather_kernel, n), out_shape=(pltpu.VMEM...]
    all_gather x1 -> x0, waiting for transfers between devices: 76.9 us -> none  [shards(): gathered = lax.all_gather(pair_block, 'blk', axis=0, tiled=True)]
    dot_general x1 -> x0, matrix products: 14.9 us -> none  [shards(): lax.dot_general(scaled, column_slab, (((0,), (0,)), ((), ())), preferred_...]
    select_n x1 -> x0, other arithmetic: 5.42 us -> none  [spread(): jnp.where(lax.axis_index(axis) == source, value, 0).astype(value.dtype)]
  transfers between devices with their start and end apart: 2 -> 0, of which waited for: 2 -> 0; matrix products, arithmetic and copies ran while one was open for 0% -> 0% of each run, Pallas kernels for 0% -> 0%
where the time goes in v1:
time: 105 us; the launch traced here: 104 us
  Pallas kernels  100 us (95%)
  between operations  1.31 us (1%)
    pallas_call x1, Pallas kernels, shards(): pl.pallas_call(functools.partial(gather_kernel, n), out_shape=(pltpu.VMEM...  96.8 us
    pallas_call x1, Pallas kernels, shards(): pl.pallas_call(finish_kernel, out_shape=jax.ShapeDtypeStruct((cols, slab)...  3.67 us

profile of v1, /device:TPU:514, one launch (start us, length us, event | category | flops | bytes accessed | tf_op | source)
XLA Modules:
  0.0 103.6 jit_solution(14754868251803637442)
XLA Ops:
  1.3 0.7 add_divide_fusion
  2.0 0.0 copy-start
  2.0 1.0 %copy-done = bf16[128,2048]{1,0:T(8,128)(2,1)S(1)} copy-done((bf16[128,2048]{1,0:T(8,128)(2,1)S(1)}, bf16[128,2048]{1,0:T(8,128)(2,1)}, u32[]{:S(2)}) %copy-start) | copy-done | bytes 524312
  3.1 96.8 %shard_map.46 = (f32[2048,1024]{1,0:T(8,128)S(1)}, bf16[2048,256]{1,0:T(8,128)(2,1)S(1)}, bf16[256,1024]{1,0:T(8,128)(2,1)S(1)}) custom-call(bf16[128,2048]{1,0:T(8,128)(2,1)S(1)} %copy-done, f32[8,256]{1,0:T(8,128)S(1)} %div.8.weight_ref), custom_call_target="tpu_custom_call" | custom-call | tf_op jit(solution)/shard_map/pallas_call | solution.py:295
  99.9 3.7 %shard_map.47 = f32[2048,1024]{1,0:T(8,128)} custom-call(f32[2048,1024]{1,0:T(8,128)S(1)} %get-tuple-element.8.acc, bf16[2048,256]{1,0:T(8,128)(2,1)S(1)} %get-tuple-element.9.lhs, bf16[256,1024]{1,0:T(8,128)(2,1)S(1)} %get-tuple-element.10.rhs), custom_call_target="tpu_custom_call" | custom-call | tf_op jit(solution)/shard_map/pallas_call | solution.py:310
  (1 shorter events, 0.0 us)
Async XLA Ops:
  2.0 1.0 %copy-start = (bf16[128,2048]{1,0:T(8,128)(2,1)S(1)}, bf16[128,2048]{1,0:T(8,128)(2,1)}, u32[]{:S(2)}) copy-start(bf16[128,2048]{1,0:T(8,128)(2,1)} %block_ref.1) | copy-start | bytes 1572868

commit v2 on v0

v2 whole, which is shorter than its diff:
```python
import functools

import jax
import jax.numpy as jnp
from jax import lax
from jax.experimental import pallas as pl
from jax.experimental.pallas import tpu as pltpu
from jax.sharding import PartitionSpec as P

MESH = pl.DeviceIdType.MESH
CORES = 2
SUB = 8
HOP = 4
LAG = 4
PASS = 2
PARTS = 2
RING = 8


def counts(n):
    total = n * SUB * 2
    return total, total // 2 + n // 2 * HOP, SUB * (n // 2 - 1) + SUB // 2


def element(e, up, row, n):
    wide = 2 * SUB
    g = e + wide // 2
    dist = g // wide
    sub = g % wide - jnp.where(dist == 0, wide // 2, 0)
    return (row + jnp.where(up, n - dist, dist)) % n, jnp.where(up, sub, wide - 1 - sub)


def schedule(n, core):
    total, end, y_count = counts(n)
    wide = 2 * SUB
    table = []
    for pos in range(n):
        ready = {0: 2}
        for d in range(1, n // 2):
            ready[d] = ready[-d] = LAG + SUB * d
        ready[n // 2] = LAG + y_count
        if pos:
            for e in range(total // 2):
                dist = (e + wide // 2) // wide
                for way in (0, 1):
                    hops = (pos, n - pos) if way == 0 else (n - pos, pos)
                    direct = e + hops[0] * HOP < end
                    tick = e + hops[0] * HOP if direct else total - 1 - e + hops[1] * HOP
                    delay = 0 if (way == core) == direct else PASS
                    key = dist if way == 0 or dist == n // 2 else -dist
                    ready[key] = max(ready[key], tick // 2 + delay)
        order = sorted(ready, key=lambda d: (ready[d], abs(d), d))
        starts, free = [], 0
        for d in order[:-1]:
            free = max(free, ready[d])
            starts.append(free)
            free += PARTS
        table.append((order, starts))
    return table


def pick(index, values):
    out = jnp.int32(values[0])
    for k in range(1, len(values)):
        out = jnp.where(index == k, jnp.int32(values[k]), out)
    return out


def gather_kernel(n, block_ref, occ_ref, virt_hbm, freq_ref, acc, last_lhs, last_rhs, held, weight, virt_ref, load_sem,
                  y_send, y_recv, d_send, d_recv, x_send, x_recv, h_send, h_recv, own_send, own_recv):
    rows, cols = block_ref.shape
    slab = cols // CORES
    tile = CORES * rows
    piece = tile // SUB
    fine = piece // 2
    tiles = cols // tile
    b = lax.axis_index("blk")
    x = lax.axis_index("col")
    core, y = b % CORES, b // CORES
    other = 1 - core
    total, end, y_count = counts(n)
    send_end = end - HOP
    pos = (x - y + n) % n

    def onward(place, way):
        return (place + jnp.where(way == 0, 1, n - 1)) % n

    peer = {"blk": y * CORES + other}
    chip_y = {"blk": onward(y, core) * CORES + core}
    chip_x = {"col": onward(x, core)}

    def own_rows(c):
        return held.at[y, pl.ds(pl.multiple_of(c * rows, rows), rows), pl.ds(0, cols)]

    load = pltpu.make_async_copy(block_ref, own_rows(core), load_sem.at[0])
    load.start()
    load_virt = pltpu.make_async_copy(virt_hbm, virt_ref, load_sem.at[1])
    load_virt.start()
    barrier = pltpu.get_barrier_semaphore()
    for device in (peer, chip_y, {"blk": onward(y, other) * CORES + core}, chip_x, {"col": onward(x, other)}):
        pl.semaphore_signal(barrier, inc=1, device_id=device, device_id_type=MESH)

    load_virt.wait()
    for k in range(n):
        virtuals = virt_ref.shape[1]
        gap = virt_ref[:, pl.ds(k * tile % virtuals, tile)] - occ_ref[k * tile // virtuals]
        weight[pl.ds(k, 1), :] = 2.0 * gap / (gap * gap + freq_ref[0] * freq_ref[0])

    pl.semaphore_wait(barrier, 5)
    load.wait()

    def copy(src, dst, send, recv, device):
        return pltpu.make_async_remote_copy(src_ref=src, dst_ref=dst, send_sem=send, recv_sem=recv,
                                            device_id=device, device_id_type=MESH)

    def own_copy(c):
        return copy(own_rows(c), own_rows(c), own_send, own_recv, peer)

    def y_piece(way, j, shift):
        d, k = j // SUB + shift, j % SUB
        chip = (y + jnp.where(way == 0, n - d, d)) % n
        at = pl.ds(pl.multiple_of(jnp.where(way == 0, k, SUB - 1 - k) * piece, piece), piece)
        return held.at[chip, at, pl.ds(0, cols)]

    def y_copy(j):
        ref = y_piece(core, j, 0)
        return copy(ref, ref, y_send.at[j % RING], y_recv.at[j], chip_y)

    def y_arrival(j):
        ref = y_piece(core, j, 1)
        return copy(ref, ref, y_send.at[j % RING], y_recv.at[j], chip_y)

    def d_copy(way, j):
        ref = y_piece(way, j, 1)
        return copy(ref, ref, d_send.at[j % RING], d_recv.at[j], peer)

    base = jnp.where(pos == 0, 0, cols)
    hops = jnp.where(core == 0, pos, (n - pos) % n)
    back = jnp.where(core == 0, (n - pos) % n, pos)

    def x_place(way, i):
        return element(jnp.where(i < total // 2, i, total - 1 - i), (i < total // 2) == (way == 0), y, n)

    def x_copy(i):
        chip, sub = x_place(core, i)
        at = pl.ds(pl.multiple_of(sub * fine, fine), fine)
        return copy(held.at[chip, at, pl.ds(pl.multiple_of(base, cols), cols)], held.at[chip, at, pl.ds(cols, cols)],
                    x_send.at[i % RING], x_recv.at[i], chip_x)

    def h_copy(way, q):
        chip, sub = x_place(way, 2 * q)
        at = pl.ds(pl.multiple_of(sub // 2 * piece, piece), piece)
        ref = held.at[chip, at, pl.ds(pl.multiple_of(cols + (1 - way) * slab, slab), slab)]
        return copy(ref, ref, h_send.at[q % RING], h_recv.at[q], peer)

    tables = [schedule(n, c) for c in range(CORES)]
    merged = [tables[c][p] for p in range(n) for c in range(CORES)]
    which = pos * CORES + core
    order = [pick(which, [o[s] for o, _ in merged]) for s in range(n)]
    starts = [pick(which, [s[k] for _, s in merged]) for k in range(n - 1)]
    prepare = LAG + 1 + y_count
    steps = max(max(s[-1] for _, s in merged) + PARTS, prepare + tiles, end // 2 + PASS)
    rhs_cols = pl.ds(pl.multiple_of(base + core * slab, slab), slab)
    final = (y + n - order[n - 1]) % n
    part = cols // PARTS

    def scaled(chip, at):
        values = held[chip, :, at].T
        return (values.astype(jnp.float32) * weight[pl.ds(chip, 1), :]).astype(jnp.bfloat16)

    def multiply(u):
        work = jnp.int32(-1)
        dist = jnp.int32(0)
        for k in range(n - 1):
            here = (u >= starts[k]) & (u < starts[k] + PARTS)
            work = jnp.where(here, u - starts[k], work)
            dist = jnp.where(here, order[k], dist)

        @pl.when(work >= 0)
        def _():
            chip = (y + n - dist) % n
            at = pl.ds(pl.multiple_of(work * part, part), part)
            acc[at, :] += jnp.dot(scaled(chip, at), held[chip, :, rhs_cols], preferred_element_type=jnp.float32)

        @pl.when((u >= prepare) & (u < prepare + tiles))
        def _():
            at = pl.ds(pl.multiple_of((u - prepare) * tile, tile), tile)
            last_lhs[at, :] = scaled(final, at)

    def x_step(t):
        i = t - hops * HOP

        @pl.when((i >= 0) & (t < end) & (hops != 0))
        def _():
            x_copy(i).wait_recv()

        @pl.when((i >= 0) & (t < send_end) & (hops != n - 1))
        def _():
            @pl.when(i >= RING)
            def _():
                x_copy(i - RING).wait_send()
            x_copy(i).start()

    own_count = SUB // CORES
    for k in range(own_count):
        y_copy(k).start()

    @pl.when(hops == 0)
    def _():
        for i in range(HOP):
            x_copy(i).start()

    own_copy(core).start()
    zero = jnp.zeros((tile, slab), jnp.float32)
    for m in range(tiles // 2):
        acc[pl.ds(m * tile, tile), :] = zero
    own_copy(other).wait_recv()
    for k in range(own_count, SUB):
        y_copy(k).start()
    for m in range(tiles // 2, tiles):
        acc[pl.ds(m * tile, tile), :] = zero

    def step(u, carry):
        j = u - LAG

        @pl.when((j >= 0) & (j < y_count))
        def _():
            y_arrival(j).wait_recv()

            @pl.when(j + SUB < y_count)
            def _():
                y_copy(j).wait_send()
                y_copy(j + SUB).start()

            @pl.when(j >= RING)
            def _():
                d_copy(core, j - RING).wait_send()
            d_copy(core, j).start()

        @pl.when((j >= 1) & (j <= y_count))
        def _():
            d_copy(other, j - 1).wait_recv()

        x_step(2 * u)
        x_step(2 * u + 1)
        q = u - hops * (HOP // 2)

        @pl.when((q >= 0) & (u < end // 2) & (hops != 0))
        def _():
            @pl.when(q >= RING)
            def _():
                h_copy(core, q - RING).wait_send()
            h_copy(core, q).start()

        r = u - PASS - back * (HOP // 2)

        @pl.when((r >= 0) & (u - PASS < end // 2) & (back != 0))
        def _():
            h_copy(other, r).wait_recv()

        multiply(u)
        return carry

    lax.fori_loop(HOP // 2, steps, step, 0)
    last_rhs[...] = held[final, :, rhs_cols]
    for k in range(1, RING + 1):
        y_copy(y_count - k).wait_send()
        d_copy(core, y_count - k).wait_send()

        @pl.when(hops != n - 1)
        def _():
            x_copy(send_end - hops * HOP - k).wait_send()

        @pl.when(hops != 0)
        def _():
            h_copy(core, end // 2 - hops * (HOP // 2) - k).wait_send()
    own_copy(core).wait_send()


def finish_kernel(acc, lhs, rhs, out_ref, staged, sems):
    tiles = sems.shape[0]
    tile = acc.shape[0] // tiles
    copies = []
    for m in range(tiles):
        at = pl.ds(m * tile, tile)
        staged[at, :] = acc[at, :] + jnp.dot(lhs[at, :], rhs[...], preferred_element_type=jnp.float32)
        out = pltpu.make_async_copy(staged.at[at], out_ref.at[at], sems.at[m])
        out.start()
        copies.append(out)
    for out in copies:
        out.wait()


def shards(pair_block, occ_energy, virt_energy, frequency):
    rows, cols = pair_block.shape
    n = lax.axis_size("col")
    assert lax.axis_size("blk") == CORES * n
    slab = cols // CORES
    tile = CORES * rows
    assert virt_energy.shape[0] % tile == 0
    total, end, y_count = counts(n)
    dma = pltpu.SemaphoreType.DMA
    vmem = pl.BlockSpec(memory_space=pltpu.VMEM)
    hbm = pl.BlockSpec(memory_space=pltpu.HBM)
    smem = pl.BlockSpec(memory_space=pltpu.SMEM)
    acc, lhs, rhs = pl.pallas_call(
        functools.partial(gather_kernel, n),
        out_shape=(pltpu.VMEM((cols, slab), jnp.float32), pltpu.VMEM((cols, tile), jnp.bfloat16),
                   pltpu.VMEM((tile, slab), jnp.bfloat16)),
        in_specs=[hbm, smem, hbm, smem],
        out_specs=(vmem, vmem, vmem),
        scratch_shapes=[
            pltpu.VMEM((n, tile, 2 * cols), jnp.bfloat16), pltpu.VMEM((n, tile), jnp.float32),
            pltpu.VMEM((1, virt_energy.shape[0]), jnp.float32), dma((2,)),
            dma((RING,)), dma((y_count,)),
            dma((RING,)), dma((y_count,)),
            dma((RING,)), dma((end,)),
            dma((RING,)), dma((end // 2,)),
            dma, dma,
        ],
        compiler_params=pltpu.CompilerParams(collective_id=0, has_side_effects=True, vmem_limit_bytes=26 * 2**20),
    )(pltpu.with_memory_space_constraint(pair_block, pltpu.HBM), occ_energy,
      pltpu.with_memory_space_constraint(virt_energy.reshape(1, -1), pltpu.HBM), frequency)
    return pl.pallas_call(
        finish_kernel,
        out_shape=jax.ShapeDtypeStruct((cols, slab), jnp.float32),
        in_specs=[vmem, vmem, vmem],
        out_specs=pl.BlockSpec(memory_space=pl.ANY),
        scratch_shapes=[pltpu.VMEM((cols, slab), jnp.float32), dma((n,))],
        compiler_params=pltpu.CompilerParams(vmem_limit_bytes=20 * 2**20),
    )(acc, lhs, rhs)


def solution(mesh):
    return jax.shard_map(
        shards,
        mesh=mesh,
        in_specs=(P(("groups", "blk"), "col"), P("groups"), P("groups"), P("groups")),
        out_specs=P(("groups", "col"), "blk"),
        check_vma=False,
    )
```

time: 223 us -> 88.7 us (0.40)
  waiting for transfers between devices: 185 us -> 0 us
  Pallas kernels: 0 us -> 85.7 us
  matrix products: 14.9 us -> 0 us
  between operations: 14.8 us -> 1.3 us
  other arithmetic: 5.43 us -> 0 us
    psum x1 -> x0, waiting for transfers between devices: 108 us -> none  [spread(): return lax.psum(kept, axis)]
    pallas_call x0 -> x2, Pallas kernels: none -> 85.7 us  [the longest x1 82 us: shards(): pl.pallas_call(functools.partial(gather_kernel, n), out_shape=(pltpu.VMEM...]
    all_gather x1 -> x0, waiting for transfers between devices: 76.9 us -> none  [shards(): gathered = lax.all_gather(pair_block, 'blk', axis=0, tiled=True)]
    dot_general x1 -> x0, matrix products: 14.9 us -> none  [shards(): lax.dot_general(scaled, column_slab, (((0,), (0,)), ((), ())), preferred_...]
    select_n x1 -> x0, other arithmetic: 5.42 us -> none  [spread(): jnp.where(lax.axis_index(axis) == source, value, 0).astype(value.dtype)]
  transfers between devices with their start and end apart: 2 -> 0, of which waited for: 2 -> 0; matrix products, arithmetic and copies ran while one was open for 0% -> 0% of each run, Pallas kernels for 0% -> 0%
where the time goes in v2:
time: 88.7 us; the launch traced here: 87 us
  Pallas kernels  85.7 us (97%)
  between operations  1.3 us (1%)
    pallas_call x1, Pallas kernels, shards(): pl.pallas_call(functools.partial(gather_kernel, n), out_shape=(pltpu.VMEM...  82 us
    pallas_call x1, Pallas kernels, shards(): pl.pallas_call(finish_kernel, out_shape=jax.ShapeDtypeStruct((cols, slab)...  3.67 us

profile of v2, /device:TPU:514, one launch (start us, length us, event | category | flops | bytes accessed | tf_op | source)
XLA Modules:
  0.0 87.0 jit_solution(11967075047953584693)
XLA Ops:
  1.3 82.0 %shard_map.46 = (f32[2048,1024]{1,0:T(8,128)S(1)}, bf16[2048,256]{1,0:T(8,128)(2,1)S(1)}, bf16[256,1024]{1,0:T(8,128)(2,1)S(1)}) custom-call(bf16[128,2048]{1,0:T(8,128)(2,1)} %block_ref.1, f32[1]{0:T(128)S(6)} %copy.5.occ_ref, f32[1,2048]{1,0:T(1,128)} %bitcast.1, f32[1]{0:T(128)S(6)} %copy.6.freq_ref), custom_call_target="tpu_custom_call" | custom-call | tf_op jit(solution)/shard_map/pallas_call | solution.py:306
  83.3 3.7 %shard_map.47 = f32[2048,1024]{1,0:T(8,128)} custom-call(f32[2048,1024]{1,0:T(8,128)S(1)} %get-tuple-element.8.acc, bf16[2048,256]{1,0:T(8,128)(2,1)S(1)} %get-tuple-element.9.lhs, bf16[256,1024]{1,0:T(8,128)(2,1)S(1)} %get-tuple-element.10.rhs), custom_call_target="tpu_custom_call" | custom-call | tf_op jit(solution)/shard_map/pallas_call | solution.py:324

commit v3 on v2

--- a/solution.py
+++ b/solution.py
@@ -13,8 +13,10 @@
 HOP = 4
 LAG = 4
 PASS = 2
-PARTS = 2
+PARTS = 4
+SHIFT = 2
 RING = 8
+PACE = 4.6
 
 
 def counts(n):
@@ -22,12 +24,28 @@
     return total, total // 2 + n // 2 * HOP, SUB * (n // 2 - 1) + SUB // 2
 
 
+def received(n, way, hops):
+    return counts(n)[1] + (SHIFT if way else -SHIFT) - hops * HOP
+
+
+def offset(hops):
+    return 2 * round(hops * PACE / 2)
+
+
+def low(value, size):
+    return value & (size - 1)
+
+
+def high(value, size):
+    return value >> (size.bit_length() - 1)
+
+
 def element(e, up, row, n):
     wide = 2 * SUB
     g = e + wide // 2
-    dist = g // wide
-    sub = g % wide - jnp.where(dist == 0, wide // 2, 0)
-    return (row + jnp.where(up, n - dist, dist)) % n, jnp.where(up, sub, wide - 1 - sub)
+    dist = high(g, wide)
+    sub = low(g, wide) - jnp.where(dist == 0, wide // 2, 0)
+    return low(row + jnp.where(up, n - dist, dist), n), jnp.where(up, sub, wide - 1 - sub)
 
 
 def schedule(n, core):
@@ -44,17 +62,17 @@
                 dist = (e + wide // 2) // wide
                 for way in (0, 1):
                     hops = (pos, n - pos) if way == 0 else (n - pos, pos)
-                    direct = e + hops[0] * HOP < end
-                    tick = e + hops[0] * HOP if direct else total - 1 - e + hops[1] * HOP
+                    direct = e < received(n, way, hops[0])
+                    tick = e + offset(hops[0]) if direct else total - 1 - e + offset(hops[1])
                     delay = 0 if (way == core) == direct else PASS
                     key = dist if way == 0 or dist == n // 2 else -dist
-                    ready[key] = max(ready[key], tick // 2 + delay)
+                    ready[key] = max(ready[key], tick // 2 + delay + 1)
         order = sorted(ready, key=lambda d: (ready[d], abs(d), d))
         starts, free = [], 0
         for d in order[:-1]:
             free = max(free, ready[d])
             starts.append(free)
-            free += PARTS
+            free += PARTS // 2
         table.append((order, starts))
     return table
 
@@ -76,14 +94,13 @@
     tiles = cols // tile
     b = lax.axis_index("blk")
     x = lax.axis_index("col")
-    core, y = b % CORES, b // CORES
+    core, y = low(b, CORES), high(b, CORES)
     other = 1 - core
     total, end, y_count = counts(n)
-    send_end = end - HOP
-    pos = (x - y + n) % n
+    pos = low(x - y + n, n)
 
     def onward(place, way):
-        return (place + jnp.where(way == 0, 1, n - 1)) % n
+        return low(place + jnp.where(way == 0, 1, n - 1), n)
 
     peer = {"blk": y * CORES + other}
     chip_y = {"blk": onward(y, core) * CORES + core}
@@ -117,41 +134,46 @@
         return copy(own_rows(c), own_rows(c), own_send, own_recv, peer)
 
     def y_piece(way, j, shift):
-        d, k = j // SUB + shift, j % SUB
-        chip = (y + jnp.where(way == 0, n - d, d)) % n
+        d, k = high(j, SUB) + shift, low(j, SUB)
+        chip = low(y + jnp.where(way == 0, n - d, d), n)
         at = pl.ds(pl.multiple_of(jnp.where(way == 0, k, SUB - 1 - k) * piece, piece), piece)
         return held.at[chip, at, pl.ds(0, cols)]
 
     def y_copy(j):
         ref = y_piece(core, j, 0)
-        return copy(ref, ref, y_send.at[j % RING], y_recv.at[j], chip_y)
+        return copy(ref, ref, y_send.at[low(j, RING)], y_recv.at[j], chip_y)
 
     def y_arrival(j):
         ref = y_piece(core, j, 1)
-        return copy(ref, ref, y_send.at[j % RING], y_recv.at[j], chip_y)
+        return copy(ref, ref, y_send.at[low(j, RING)], y_recv.at[j], chip_y)
 
     def d_copy(way, j):
         ref = y_piece(way, j, 1)
-        return copy(ref, ref, d_send.at[j % RING], d_recv.at[j], peer)
+        return copy(ref, ref, d_send.at[low(j, RING)], d_recv.at[j], peer)
 
     base = jnp.where(pos == 0, 0, cols)
-    hops = jnp.where(core == 0, pos, (n - pos) % n)
-    back = jnp.where(core == 0, (n - pos) % n, pos)
+    hops = jnp.where(core == 0, pos, low(n - pos, n))
+    back = jnp.where(core == 0, low(n - pos, n), pos)
+    wait_off = pick(hops, [offset(h) for h in range(n)])
+    back_off = pick(back, [offset(h) for h in range(n)])
+    arriving = jnp.where(hops == 0, 0, received(n, 1, hops) - jnp.where(core == 0, 2 * SHIFT, 0))
+    leaving = jnp.where(hops == n - 1, 0, received(n, 1, hops + 1) - jnp.where(core == 0, 2 * SHIFT, 0))
+    handed = jnp.where(back == 0, 0, received(n, 1, back) - jnp.where(core == 1, 2 * SHIFT, 0))
 
     def x_place(way, i):
         return element(jnp.where(i < total // 2, i, total - 1 - i), (i < total // 2) == (way == 0), y, n)
 
-    def x_copy(i):
-        chip, sub = x_place(core, i)
-        at = pl.ds(pl.multiple_of(sub * fine, fine), fine)
+    def x_copy(i, place, second):
+        chip, sub = place
+        at = pl.ds(pl.multiple_of((sub ^ second) * fine, fine), fine)
         return copy(held.at[chip, at, pl.ds(pl.multiple_of(base, cols), cols)], held.at[chip, at, pl.ds(cols, cols)],
-                    x_send.at[i % RING], x_recv.at[i], chip_x)
-
-    def h_copy(way, q):
-        chip, sub = x_place(way, 2 * q)
-        at = pl.ds(pl.multiple_of(sub // 2 * piece, piece), piece)
+                    x_send.at[low(i, RING)], x_recv.at[i], chip_x)
+
+    def h_copy(way, q, place):
+        chip, sub = place
+        at = pl.ds(pl.multiple_of(high(sub, 2) * piece, piece), piece)
         ref = held.at[chip, at, pl.ds(pl.multiple_of(cols + (1 - way) * slab, slab), slab)]
-        return copy(ref, ref, h_send.at[q % RING], h_recv.at[q], peer)
+        return copy(ref, ref, h_send.at[low(q, RING)], h_recv.at[q], peer)
 
     tables = [schedule(n, c) for c in range(CORES)]
     merged = [tables[c][p] for p in range(n) for c in range(CORES)]
@@ -159,47 +181,36 @@
     order = [pick(which, [o[s] for o, _ in merged]) for s in range(n)]
     starts = [pick(which, [s[k] for _, s in merged]) for k in range(n - 1)]
     prepare = LAG + 1 + y_count
-    steps = max(max(s[-1] for _, s in merged) + PARTS, prepare + tiles, end // 2 + PASS)
+    steps = max(max(s[-1] for _, s in merged) + PARTS // 2, prepare + tiles,
+                max(received(n, w, h) + offset(h) for w in (0, 1) for h in range(1, n)) // 2 + PASS)
     rhs_cols = pl.ds(pl.multiple_of(base + core * slab, slab), slab)
-    final = (y + n - order[n - 1]) % n
+    final = low(y + n - order[n - 1], n)
     part = cols // PARTS
 
     def scaled(chip, at):
         values = held[chip, :, at].T
         return (values.astype(jnp.float32) * weight[pl.ds(chip, 1), :]).astype(jnp.bfloat16)
 
-    def multiply(u):
+    def due(u):
         work = jnp.int32(-1)
         dist = jnp.int32(0)
         for k in range(n - 1):
-            here = (u >= starts[k]) & (u < starts[k] + PARTS)
+            here = (u >= starts[k]) & (u < starts[k] + PARTS // 2)
             work = jnp.where(here, u - starts[k], work)
             dist = jnp.where(here, order[k], dist)
-
+        return work, low(y + n - dist, n)
+
+    def multiply(work, chip, second):
         @pl.when(work >= 0)
         def _():
-            chip = (y + n - dist) % n
-            at = pl.ds(pl.multiple_of(work * part, part), part)
+            at = pl.ds(pl.multiple_of((2 * work + second) * part, part), part)
             acc[at, :] += jnp.dot(scaled(chip, at), held[chip, :, rhs_cols], preferred_element_type=jnp.float32)
 
+    def prepare_last(u):
         @pl.when((u >= prepare) & (u < prepare + tiles))
         def _():
             at = pl.ds(pl.multiple_of((u - prepare) * tile, tile), tile)
             last_lhs[at, :] = scaled(final, at)
-
-    def x_step(t):
-        i = t - hops * HOP
-
-        @pl.when((i >= 0) & (t < end) & (hops != 0))
-        def _():
-            x_copy(i).wait_recv()
-
-        @pl.when((i >= 0) & (t < send_end) & (hops != n - 1))
-        def _():
-            @pl.when(i >= RING)
-            def _():
-                x_copy(i - RING).wait_send()
-            x_copy(i).start()
 
     own_count = SUB // CORES
     for k in range(own_count):
@@ -208,7 +219,7 @@
     @pl.when(hops == 0)
     def _():
         for i in range(HOP):
-            x_copy(i).start()
+            x_copy(i, x_place(core, jnp.int32(i - i % 2)), i % 2).start()
 
     own_copy(core).start()
     zero = jnp.zeros((tile, slab), jnp.float32)
@@ -241,39 +252,57 @@
         def _():
             d_copy(other, j - 1).wait_recv()
 
-        x_step(2 * u)
-        x_step(2 * u + 1)
-        q = u - hops * (HOP // 2)
-
-        @pl.when((q >= 0) & (u < end // 2) & (hops != 0))
+        work, chip = due(u)
+        i = 2 * u - wait_off
+        place = x_place(core, i)
+        for second in (0, 1):
+            @pl.when((i >= 0) & (i < arriving))
+            def _():
+                x_copy(i + second, place, second).wait_recv()
+
+            @pl.when((i >= 0) & (i < leaving))
+            def _():
+                @pl.when(i >= RING)
+                def _():
+                    x_copy(i + second - RING, place, second).wait_send()
+                x_copy(i + second, place, second).start()
+
+            if second == 0:
+                multiply(work, chip, 0)
+
+        q = u - high(wait_off, 2)
+
+        @pl.when((q >= 0) & (i < arriving))
         def _():
             @pl.when(q >= RING)
             def _():
-                h_copy(core, q - RING).wait_send()
-            h_copy(core, q).start()
-
-        r = u - PASS - back * (HOP // 2)
-
-        @pl.when((r >= 0) & (u - PASS < end // 2) & (back != 0))
-        def _():
-            h_copy(other, r).wait_recv()
-
-        multiply(u)
+                h_copy(core, q - RING, place).wait_send()
+            h_copy(core, q, place).start()
+
+        r = u - PASS - high(back_off, 2)
+
+        @pl.when((r >= 0) & (2 * r < handed))
+        def _():
+            h_copy(other, r, x_place(other, 2 * r)).wait_recv()
+
+        multiply(work, chip, 1)
+        prepare_last(u)
         return carry
 
     lax.fori_loop(HOP // 2, steps, step, 0)
     last_rhs[...] = held[final, :, rhs_cols]
+    here = (y, jnp.int32(0))
     for k in range(1, RING + 1):
         y_copy(y_count - k).wait_send()
         d_copy(core, y_count - k).wait_send()
 
-        @pl.when(hops != n - 1)
-        def _():
-            x_copy(send_end - hops * HOP - k).wait_send()
-
-        @pl.when(hops != 0)
-        def _():
-            h_copy(core, end // 2 - hops * (HOP // 2) - k).wait_send()
+        @pl.when(leaving > 0)
+        def _():
+            x_copy(leaving - k, here, 0).wait_send()
+
+        @pl.when(arriving > 0)
+        def _():
+            h_copy(core, high(arriving, 2) - k, here).wait_send()
     own_copy(core).wait_send()
 
 
@@ -314,8 +343,8 @@
             pltpu.VMEM((1, virt_energy.shape[0]), jnp.float32), dma((2,)),
             dma((RING,)), dma((y_count,)),
             dma((RING,)), dma((y_count,)),
-            dma((RING,)), dma((end,)),
-            dma((RING,)), dma((end // 2,)),
+            dma((RING,)), dma((end + SHIFT,)),
+            dma((RING,)), dma(((end + SHIFT) // 2,)),
             dma, dma,
         ],
         compiler_params=pltpu.CompilerParams(collective_id=0, has_side_effects=True, vmem_limit_bytes=26 * 2**20),

time: 88.7 us -> 87.5 us (0.986)
  no operation moved by 1% of the time
where the time goes in v3:
time: 87.5 us; the launch traced here: 86.3 us
  Pallas kernels  85 us (97%)
  between operations  1.3 us (1%)
    pallas_call x1, Pallas kernels, shards(): pl.pallas_call(functools.partial(gather_kernel, n), out_shape=(pltpu.VMEM...  81.4 us
    pallas_call x1, Pallas kernels, shards(): pl.pallas_call(finish_kernel, out_shape=jax.ShapeDtypeStruct((cols, slab)...  3.67 us

profile of v3, /device:TPU:514, one launch (start us, length us, event | category | flops | bytes accessed | tf_op | source)
XLA Modules:
  0.0 86.3 jit_solution(7011795702155200897)
XLA Ops:
  1.3 81.4 %shard_map.46 = (f32[2048,1024]{1,0:T(8,128)S(1)}, bf16[2048,256]{1,0:T(8,128)(2,1)S(1)}, bf16[256,1024]{1,0:T(8,128)(2,1)S(1)}) custom-call(bf16[128,2048]{1,0:T(8,128)(2,1)} %block_ref.1, f32[1]{0:T(128)S(6)} %copy.5.occ_ref, f32[1,2048]{1,0:T(1,128)} %bitcast.1, f32[1]{0:T(128)S(6)} %copy.6.freq_ref), custom_call_target="tpu_custom_call" | custom-call | tf_op jit(solution)/shard_map/pallas_call | solution.py:335
  82.7 3.7 %shard_map.47 = f32[2048,1024]{1,0:T(8,128)} custom-call(f32[2048,1024]{1,0:T(8,128)S(1)} %get-tuple-element.8.acc, bf16[2048,256]{1,0:T(8,128)(2,1)S(1)} %get-tuple-element.9.lhs, bf16[256,1024]{1,0:T(8,128)(2,1)S(1)} %get-tuple-element.10.rhs), custom_call_target="tpu_custom_call" | custom-call | tf_op jit(solution)/shard_map/pallas_call | solution.py:353

commit v4 on v3

--- a/solution.py
+++ b/solution.py
@@ -10,17 +10,21 @@
 MESH = pl.DeviceIdType.MESH
 CORES = 2
 SUB = 8
+FINE = 2
 HOP = 4
 LAG = 4
 PASS = 2
 PARTS = 4
 SHIFT = 2
 RING = 8
-PACE = 4.6
+X_RING = 8
+PACE = 2.0
+PARTNER_PACE = 2.4
+EASE = 4
 
 
 def counts(n):
-    total = n * SUB * 2
+    total = n * SUB * FINE
     return total, total // 2 + n // 2 * HOP, SUB * (n // 2 - 1) + SUB // 2
 
 
@@ -28,8 +32,8 @@
     return counts(n)[1] + (SHIFT if way else -SHIFT) - hops * HOP
 
 
-def offset(hops):
-    return 2 * round(hops * PACE / 2)
+def offset(hops, pace=PACE):
+    return FINE * round(hops * pace)
 
 
 def low(value, size):
@@ -41,7 +45,7 @@
 
 
 def element(e, up, row, n):
-    wide = 2 * SUB
+    wide = FINE * SUB
     g = e + wide // 2
     dist = high(g, wide)
     sub = low(g, wide) - jnp.where(dist == 0, wide // 2, 0)
@@ -50,23 +54,25 @@
 
 def schedule(n, core):
     total, end, y_count = counts(n)
-    wide = 2 * SUB
+    wide = FINE * SUB
     table = []
     for pos in range(n):
         ready = {0: 2}
         for d in range(1, n // 2):
-            ready[d] = ready[-d] = LAG + SUB * d
-        ready[n // 2] = LAG + y_count
+            ready[d] = ready[-d] = LAG + SUB * d - 1 + (EASE if pos else 1)
+        ready[n // 2] = LAG + y_count - 1 + (EASE if pos else 1)
         if pos:
             for e in range(total // 2):
                 dist = (e + wide // 2) // wide
                 for way in (0, 1):
                     hops = (pos, n - pos) if way == 0 else (n - pos, pos)
                     direct = e < received(n, way, hops[0])
-                    tick = e + offset(hops[0]) if direct else total - 1 - e + offset(hops[1])
-                    delay = 0 if (way == core) == direct else PASS
+                    mine = (way == core) == direct
+                    hop = hops[0] if direct else hops[1]
+                    tick = (e if direct else total - 1 - e) + offset(hop, PACE if mine else PARTNER_PACE)
+                    delay = 0 if mine else PASS
                     key = dist if way == 0 or dist == n // 2 else -dist
-                    ready[key] = max(ready[key], tick // 2 + delay + 1)
+                    ready[key] = max(ready[key], tick // FINE + delay + 1)
         order = sorted(ready, key=lambda d: (ready[d], abs(d), d))
         starts, free = [], 0
         for d in order[:-1]:
@@ -90,7 +96,7 @@
     slab = cols // CORES
     tile = CORES * rows
     piece = tile // SUB
-    fine = piece // 2
+    fine = piece // FINE
     tiles = cols // tile
     b = lax.axis_index("blk")
     x = lax.axis_index("col")
@@ -155,7 +161,7 @@
     hops = jnp.where(core == 0, pos, low(n - pos, n))
     back = jnp.where(core == 0, low(n - pos, n), pos)
     wait_off = pick(hops, [offset(h) for h in range(n)])
-    back_off = pick(back, [offset(h) for h in range(n)])
+    back_off = pick(back, [offset(h, PARTNER_PACE) for h in range(n)])
     arriving = jnp.where(hops == 0, 0, received(n, 1, hops) - jnp.where(core == 0, 2 * SHIFT, 0))
     leaving = jnp.where(hops == n - 1, 0, received(n, 1, hops + 1) - jnp.where(core == 0, 2 * SHIFT, 0))
     handed = jnp.where(back == 0, 0, received(n, 1, back) - jnp.where(core == 1, 2 * SHIFT, 0))
@@ -167,11 +173,11 @@
         chip, sub = place
         at = pl.ds(pl.multiple_of((sub ^ second) * fine, fine), fine)
         return copy(held.at[chip, at, pl.ds(pl.multiple_of(base, cols), cols)], held.at[chip, at, pl.ds(cols, cols)],
-                    x_send.at[low(i, RING)], x_recv.at[i], chip_x)
+                    x_send.at[low(i, X_RING)], x_recv.at[i], chip_x)
 
     def h_copy(way, q, place):
         chip, sub = place
-        at = pl.ds(pl.multiple_of(high(sub, 2) * piece, piece), piece)
+        at = pl.ds(pl.multiple_of(high(sub, FINE) * piece, piece), piece)
         ref = held.at[chip, at, pl.ds(pl.multiple_of(cols + (1 - way) * slab, slab), slab)]
         return copy(ref, ref, h_send.at[low(q, RING)], h_recv.at[q], peer)
 
@@ -180,9 +186,20 @@
     which = pos * CORES + core
     order = [pick(which, [o[s] for o, _ in merged]) for s in range(n)]
     starts = [pick(which, [s[k] for _, s in merged]) for k in range(n - 1)]
-    prepare = LAG + 1 + y_count
-    steps = max(max(s[-1] for _, s in merged) + PARTS // 2, prepare + tiles,
-                max(received(n, w, h) + offset(h) for w in (0, 1) for h in range(1, n)) // 2 + PASS)
+    prepare = LAG + EASE + y_count
+    last = []
+    for p in range(n):
+        for c in range(CORES):
+            mine, theirs = (p, (n - p) % n) if c == 0 else ((n - p) % n, p)
+            step_ends = [tables[c][p][1][-1] + PARTS // 2, prepare + tiles // 2]
+            if mine < n - 1:
+                step_ends.append((received(n, c, mine + 1) + offset(mine)) // FINE)
+            if mine:
+                step_ends.append((received(n, c, mine) + offset(mine)) // FINE)
+            if theirs:
+                step_ends.append((received(n, 1 - c, theirs) + offset(theirs, PARTNER_PACE)) // FINE + PASS)
+            last.append(max(step_ends))
+    steps = pick(which, last)
     rhs_cols = pl.ds(pl.multiple_of(base + core * slab, slab), slab)
     final = low(y + n - order[n - 1], n)
     part = cols // PARTS
@@ -207,19 +224,21 @@
             acc[at, :] += jnp.dot(scaled(chip, at), held[chip, :, rhs_cols], preferred_element_type=jnp.float32)
 
     def prepare_last(u):
-        @pl.when((u >= prepare) & (u < prepare + tiles))
-        def _():
-            at = pl.ds(pl.multiple_of((u - prepare) * tile, tile), tile)
-            last_lhs[at, :] = scaled(final, at)
+        @pl.when((u >= prepare) & (u < prepare + tiles // 2))
+        def _():
+            for k in (0, 1):
+                at = pl.ds(pl.multiple_of((2 * (u - prepare) + k) * tile, tile), tile)
+                last_lhs[at, :] = scaled(final, at)
 
     own_count = SUB // CORES
+    ease = jnp.where(pos == 0, 1, EASE)
     for k in range(own_count):
         y_copy(k).start()
 
     @pl.when(hops == 0)
     def _():
         for i in range(HOP):
-            x_copy(i, x_place(core, jnp.int32(i - i % 2)), i % 2).start()
+            x_copy(i, x_place(core, jnp.int32(i - i % FINE)), i % FINE).start()
 
     own_copy(core).start()
     zero = jnp.zeros((tile, slab), jnp.float32)
@@ -248,29 +267,31 @@
                 d_copy(core, j - RING).wait_send()
             d_copy(core, j).start()
 
-        @pl.when((j >= 1) & (j <= y_count))
-        def _():
-            d_copy(other, j - 1).wait_recv()
+        given = j - ease
+
+        @pl.when((given >= 0) & (given < y_count))
+        def _():
+            d_copy(other, given).wait_recv()
 
         work, chip = due(u)
-        i = 2 * u - wait_off
+        i = FINE * u - wait_off
         place = x_place(core, i)
-        for second in (0, 1):
+        for second in range(FINE):
             @pl.when((i >= 0) & (i < arriving))
             def _():
                 x_copy(i + second, place, second).wait_recv()
 
             @pl.when((i >= 0) & (i < leaving))
             def _():
-                @pl.when(i >= RING)
+                @pl.when(i >= X_RING)
                 def _():
-                    x_copy(i + second - RING, place, second).wait_send()
+                    x_copy(i + second - X_RING, place, second).wait_send()
                 x_copy(i + second, place, second).start()
 
-            if second == 0:
+            if second == FINE // 2 - 1:
                 multiply(work, chip, 0)
 
-        q = u - high(wait_off, 2)
+        q = u - high(wait_off, FINE)
 
         @pl.when((q >= 0) & (i < arriving))
         def _():
@@ -279,30 +300,30 @@
                 h_copy(core, q - RING, place).wait_send()
             h_copy(core, q, place).start()
 
-        r = u - PASS - high(back_off, 2)
-
-        @pl.when((r >= 0) & (2 * r < handed))
-        def _():
-            h_copy(other, r, x_place(other, 2 * r)).wait_recv()
+        r = u - PASS - high(back_off, FINE)
+
+        @pl.when((r >= 0) & (FINE * r < handed))
+        def _():
+            h_copy(other, r, x_place(other, FINE * r)).wait_recv()
 
         multiply(work, chip, 1)
         prepare_last(u)
         return carry
 
-    lax.fori_loop(HOP // 2, steps, step, 0)
+    lax.fori_loop(HOP // FINE, steps, step, 0)
     last_rhs[...] = held[final, :, rhs_cols]
     here = (y, jnp.int32(0))
     for k in range(1, RING + 1):
         y_copy(y_count - k).wait_send()
         d_copy(core, y_count - k).wait_send()
 
+        @pl.when(arriving > 0)
+        def _():
+            h_copy(core, high(arriving, FINE) - k, here).wait_send()
+    for k in range(1, X_RING + 1):
         @pl.when(leaving > 0)
         def _():
             x_copy(leaving - k, here, 0).wait_send()
-
-        @pl.when(arriving > 0)
-        def _():
-            h_copy(core, high(arriving, 2) - k, here).wait_send()
     own_copy(core).wait_send()
 
 
@@ -343,8 +364,8 @@
             pltpu.VMEM((1, virt_energy.shape[0]), jnp.float32), dma((2,)),
             dma((RING,)), dma((y_count,)),
             dma((RING,)), dma((y_count,)),
-            dma((RING,)), dma((end + SHIFT,)),
-            dma((RING,)), dma(((end + SHIFT) // 2,)),
+            dma((X_RING,)), dma((end + SHIFT,)),
+            dma((RING,)), dma(((end + SHIFT) // FINE,)),
             dma, dma,
         ],
         compiler_params=pltpu.CompilerParams(collective_id=0, has_side_effects=True, vmem_limit_bytes=26 * 2**20),

time: 87.5 us -> 85.5 us (0.977); the launches traced: 86.3 us -> 85.4 us
  Pallas kernels: 85 us -> 84.1 us
    pallas_call x1, Pallas kernels: 81.4 us -> 80.4 us  [shards(): pl.pallas_call(functools.partial(gather_kernel, n), out_shape=(pltpu.VMEM...]
where the time goes in v4:
time: 85.5 us; the launch traced here: 85.4 us
  Pallas kernels  84.1 us (98%)
  between operations  1.3 us (2%)
    pallas_call x1, Pallas kernels, shards(): pl.pallas_call(functools.partial(gather_kernel, n), out_shape=(pltpu.VMEM...  80.4 us
    pallas_call x1, Pallas kernels, shards(): pl.pallas_call(finish_kernel, out_shape=jax.ShapeDtypeStruct((cols, slab)...  3.67 us

profile of v4, /device:TPU:514, one launch (start us, length us, event | category | flops | bytes accessed | tf_op | source)
XLA Modules:
  0.0 85.4 jit_solution(1371084215470787472)
XLA Ops:
  1.3 80.4 %shard_map.46 = (f32[2048,1024]{1,0:T(8,128)S(1)}, bf16[2048,256]{1,0:T(8,128)(2,1)S(1)}, bf16[256,1024]{1,0:T(8,128)(2,1)S(1)}) custom-call(bf16[128,2048]{1,0:T(8,128)(2,1)} %block_ref.1, f32[1]{0:T(128)S(6)} %copy.5.occ_ref, f32[1,2048]{1,0:T(1,128)} %bitcast.1, f32[1]{0:T(128)S(6)} %copy.6.freq_ref), custom_call_target="tpu_custom_call" | custom-call | tf_op jit(solution)/shard_map/pallas_call | solution.py:356
  81.7 3.7 %shard_map.47 = f32[2048,1024]{1,0:T(8,128)} custom-call(f32[2048,1024]{1,0:T(8,128)S(1)} %get-tuple-element.8.acc, bf16[2048,256]{1,0:T(8,128)(2,1)S(1)} %get-tuple-element.9.lhs, bf16[256,1024]{1,0:T(8,128)(2,1)S(1)} %get-tuple-element.10.rhs), custom_call_target="tpu_custom_call" | custom-call | tf_op jit(solution)/shard_map/pallas_call | solution.py:374

commit v5 on v4

--- a/solution.py
+++ b/solution.py
@@ -13,13 +13,13 @@
 FINE = 2
 HOP = 4
 LAG = 4
-PASS = 2
+PASS = 1
 PARTS = 4
-SHIFT = 2
+SHIFT = 4
 RING = 8
 X_RING = 8
 PACE = 2.0
-PARTNER_PACE = 2.4
+PARTNER_PACE = 2.5
 EASE = 4
 
 

time: 85.5 us -> 85.6 us (level)
  no operation moved by 1% of the time
where the time goes in v5:
time: 85.6 us; the launch traced here: 85.3 us
  Pallas kernels  84 us (98%)
  between operations  1.3 us (2%)
    pallas_call x1, Pallas kernels, shards(): pl.pallas_call(functools.partial(gather_kernel, n), out_shape=(pltpu.VMEM...  80.3 us
    pallas_call x1, Pallas kernels, shards(): pl.pallas_call(finish_kernel, out_shape=jax.ShapeDtypeStruct((cols, slab)...  3.67 us

profile of v5, /device:TPU:514, one launch (start us, length us, event | category | flops | bytes accessed | tf_op | source)
XLA Modules:
  0.0 85.3 jit_solution(15099643197422387865)
XLA Ops:
  1.3 80.3 %shard_map.46 = (f32[2048,1024]{1,0:T(8,128)S(1)}, bf16[2048,256]{1,0:T(8,128)(2,1)S(1)}, bf16[256,1024]{1,0:T(8,128)(2,1)S(1)}) custom-call(bf16[128,2048]{1,0:T(8,128)(2,1)} %block_ref.1, f32[1]{0:T(128)S(6)} %copy.5.occ_ref, f32[1,2048]{1,0:T(1,128)} %bitcast.1, f32[1]{0:T(128)S(6)} %copy.6.freq_ref), custom_call_target="tpu_custom_call" | custom-call | tf_op jit(solution)/shard_map/pallas_call | solution.py:356
  81.6 3.7 %shard_map.47 = f32[2048,1024]{1,0:T(8,128)} custom-call(f32[2048,1024]{1,0:T(8,128)S(1)} %get-tuple-element.8.acc, bf16[2048,256]{1,0:T(8,128)(2,1)S(1)} %get-tuple-element.9.lhs, bf16[256,1024]{1,0:T(8,128)(2,1)S(1)} %get-tuple-element.10.rhs), custom_call_target="tpu_custom_call" | custom-call | tf_op jit(solution)/shard_map/pallas_call | solution.py:374
